TPU v7x, 32 devices: a whole 2x2x4 slice. The times are simulated.
32 devices in a mesh: row: 8 (over z, x), col: 4 (over y, core).
Axes of the slice: x: 2, y: 2, z: 4, core: 2. Of those that a mesh axis runs over, the one named last changes fastest.
Arguments:
- coeffs: bfloat16 [1024, 128, 128], P(('row', 'col')), as said below
- tiles: int32 [1024, 1], replicated, may hold values from 0 to 7; in each aligned block of 32 rows (0 to 31, 32 to 63, ...) at most 5 rows name the same one
- primal: bfloat16 [1024, 1024], replicated, as said below
- dual_inverse: bfloat16 [1024, 1024], replicated, as said below
Outputs:
- schur: float32 [1024, 1024], P('row', 'col')
Inputs may be any that keep to these rules, and one draw needn't show every extreme that they name: `tiles`: within each aligned block of 32 constraints (the constraints of one device) no tile is named more than 5 times, a bound that some block reaches. Each coeffs[i] is symmetric. `primal`: Symmetric. `dual_inverse`: Symmetric.
All inputs are finite; a program needn't handle non-finite values.
Results may differ from a plain program's by a relative error of at most 0.0022.
Values may be sent and summed in bfloat16 or wider, within the bound.
A program may use at most 128 MiB of HBM per device.

v0:
```python
import jax
import jax.numpy as jnp
from jax import lax
from jax.sharding import PartitionSpec as P

MOST = 5


def slot_ranks(tile_group, first_tile, tile_width):
    labels = first_tile + jnp.arange(tile_width, dtype=jnp.int32)
    member = (tile_group[:, :, None] == labels[None, None, :]).astype(jnp.int32)
    before = jnp.cumsum(member, axis=1) - member
    return (member, jnp.sum(before * member, axis=2))


def slot_picks(tile_group, first_tile, tile_width, slot_depth):
    member, ordinal = slot_ranks(tile_group, first_tile, tile_width)
    levels = jnp.arange(slot_depth, dtype=jnp.int32)
    chosen = member[:, :, :, None] * (
        ordinal[:, :, None, None] == levels[None, None, None, :]
    ).astype(jnp.int32)
    return jnp.transpose(chosen, (0, 2, 3, 1)).astype(jnp.bfloat16)


def shards(coeffs, tiles, primal, dual_inverse):
    col_size = lax.axis_size("col")
    row_size = lax.axis_size("row")
    col_index = lax.axis_index("col")
    row_index = lax.axis_index("row")
    own_count = coeffs.shape[0]
    tile_size = coeffs.shape[1]
    tile_count = primal.shape[0] // tile_size
    per_col = tile_count // col_size
    slot_depth = MOST
    tile_area = tile_size * tile_size
    tile_ids = tiles[:, 0]
    row_count = col_size * own_count
    first_tile = col_index * per_col
    row_coeffs = lax.all_gather(coeffs, "col", axis=0, tiled=True)
    row_tiles = lax.dynamic_slice_in_dim(tile_ids, row_index * row_count, row_count)
    primal_strip = lax.dynamic_slice_in_dim(primal, first_tile * tile_size, per_col * tile_size, 1)
    primal_strip = primal_strip.reshape(tile_count, tile_size, per_col, tile_size)
    primal_pick = jnp.take(primal_strip, row_tiles, axis=0)
    product_tile = jnp.einsum(
        "iab,ibvc->ivac", row_coeffs, primal_pick, preferred_element_type=jnp.float32
    ).astype(jnp.bfloat16)
    dual_strip = lax.dynamic_slice_in_dim(
        dual_inverse, first_tile * tile_size, per_col * tile_size, 0
    )
    dual_strip = dual_strip.reshape(per_col, tile_size, tile_count, tile_size)
    dual_pick = jnp.take(dual_strip, row_tiles, axis=2)
    reduced = jnp.einsum(
        "ivba,vcib->ivac", product_tile, dual_pick, preferred_element_type=jnp.float32
    ).astype(jnp.bfloat16)
    reduced = reduced.reshape(row_count, per_col, tile_area)
    chosen_slots = slot_picks(
        row_tiles.reshape(col_size, own_count), first_tile, per_col, slot_depth
    )
    routed = jnp.einsum(
        "gvqk,gkx->gvqx",
        chosen_slots,
        row_coeffs.reshape(col_size, own_count, tile_area),
        preferred_element_type=jnp.float32,
    ).astype(jnp.bfloat16)
    values = jnp.einsum(
        "ivx,svqx->isvq",
        reduced,
        lax.all_gather(routed, "row", axis=0, tiled=True),
        preferred_element_type=jnp.float32,
    )
    home_span = row_size * per_col * slot_depth
    values = values.reshape(row_count, col_size, home_span)
    landed = lax.all_to_all(values, "col", split_axis=1, concat_axis=1, tiled=True)
    landed = landed.reshape(row_count, col_size * home_span)
    home_tiles = lax.dynamic_slice_in_dim(
        tile_ids, col_index * row_size * own_count, row_size * own_count
    )
    home_tiles = home_tiles.reshape(row_size, own_count)
    member, ordinal = slot_ranks(home_tiles, 0, tile_count)
    owner_col = home_tiles // per_col
    within = home_tiles - owner_col * per_col
    sender = jnp.arange(row_size, dtype=jnp.int32)[:, None]
    column_pick = (
        owner_col * home_span + sender * (per_col * slot_depth) + within * slot_depth + ordinal
    )
    return jnp.take(landed, column_pick.reshape(-1), axis=1)


def solution(mesh):
    return jax.shard_map(
        shards,
        mesh=mesh,
        in_specs=(P(("row", "col"), None, None), P(), P(), P()),
        out_specs=P("row", "col"),
        check_vma=False,
    )
```

profile of v0, /device:TPU:0, one launch (start us, length us, event | category | flops | bytes accessed | tf_op | source)
XLA Modules:
  0.0 243.5 jit_solution(329211813767962392)
XLA Ops:
  6.5 0.0 copy-start
  6.5 0.0 all-gather.3.cloned.1.call-start
  6.5 0.7 all-gather.3.cloned.1.call-update
  7.3 0.0 all-gather.5.cloned.1.call-start
  7.3 0.7 fusion.41
  8.0 0.1 eq.64
  8.1 0.1 compare_convert_fusion
  8.2 0.1 reduce_window_sum.23
  8.2 0.2 fusion.35
  8.5 0.1 compare_convert_fusion.1
  8.5 37.6 %all-gather.3.cloned.1.call-done = bf16[128,128,128]{2,1,0:T(8,128)(2,1)} async-done(((bf16[32,128,128]{2,1,0:T(8,128)(2,1)}), bf16[128,128,128]{2,1,0:T(8,128)(2,1)}) %all-gather.3.cloned.1.call-update) | async-done | bytes 4194320 | tf_op jit(solution)/shard_map/all_gather | solution.py:39
  46.1 7.3 %reshape.93 = bf16[4,32,16384,1]{2,1,0,3:T(8,128)(2,1)} reshape(bf16[128,128,128]{2,1,0:T(8,128)(2,1)} %all-gather.3.cloned.1.call-done) | data formatting | bytes 8388608 | tf_op jit(solution)/shard_map/reshape | solution.py:62
  53.4 0.0 copy-start.1
  53.4 2.9 %convolution_convert_fusion = bf16[4,2,5,16384]{3,2,1,0:T(8,128)(2,1)S(1)} fusion(bf16[4,32,16384,1]{2,1,0,3:T(8,128)(2,1)} %reshape.93, s32[4,5,32]{2,1,0:T(8,128)S(1)} %fusion.39, s32[4,2,32]{2,1,0:T(2,128)S(1)} %compare_convert_fusion.1), kind=kOutput, calls=%fused_computation.3 | convolution fusion | flops 42600960 | bytes 5508608 | tf_op jit(solution)/shard_map/gvqk,gkx->gvqx/dot_general | solution.py:59
  56.3 2.6 %copy.45 = bf16[4,2,5,16384]{3,1,2,0:T(2,128)(2,1)} copy(bf16[4,2,5,16384]{3,2,1,0:T(8,128)(2,1)S(1)} %convolution_convert_fusion) | data formatting | bytes 2621440 | tf_op jit(solution)/shard_map/convert_element_type | solution.py:64
  58.9 0.0 all-gather.5.cloned.1.call-update
  58.9 0.0 copy-done
  58.9 0.1 constant_dynamic-slice_fusion
  59.0 0.1 reshape.97
  59.2 0.1 copy.47
  59.3 1.1 dynamic-slice_bitcast_fusion
  60.3 0.1 copy.62
  60.4 0.1 copy.49
  60.5 0.0 copy-done.1
  60.6 6.7 %gather_fusion = bf16[128,128,2,128]{3,1,2,0:T(8,128)(2,1)} fusion(bf16[8,128,2,128]{3,1,2,0:T(8,128)(2,1)S(1)} %copy.47, s32[1024]{0:T(1024)S(1)} %pad_clamp_fusion.1), kind=kCustom, calls=%fused_computation | custom fusion | bytes 16777728 | tf_op jit(solution)/shard_map/jit(_take)/gather | solution.py:43
  67.3 6.7 %gather_fusion.1 = bf16[128,2,128,128]{3,2,1,0:T(8,128)(2,1)} fusion(bf16[2,128,8,128]{3,1,2,0:T(8,128)(2,1)S(1)} %copy.49, s32[1024]{0:T(1024)S(1)} %pad_clamp_fusion.1), kind=kCustom, calls=%fused_computation.1 | custom fusion | bytes 16777728 | tf_op jit(solution)/shard_map/jit(_take)/gather | solution.py:51
  74.0 0.1 eq.60
  74.1 0.1 copy.43
  74.1 0.7 fusion.44
  74.9 0.1 copy.44
  75.0 0.1 reduce_sum.21
  75.0 0.1 add.72
  75.1 0.1 add.73
  75.2 15.0 %fusion.11 = bf16[128,2,128,128]{3,2,1,0:T(8,128)(2,1)} fusion(bf16[128,2,128,128]{3,2,1,0:T(8,128)(2,1)} %gather_fusion.1, pred[128]{0:T(512)(128)(4,1)S(1)} %get-tuple-element.7, bf16[128,128,2,128]{3,1,2,0:T(8,128)(2,1)} %gather_fusion, bf16[128,128,128]{2,1,0:T(8,128)(2,1)} %all-gather.3.cloned.1.call-done), kind=kOutput, calls=%fused_computation.15 | convolution fusion | flops 2164260864 | bytes 29360256 | tf_op jit(solution)/shard_map/ivba,vcib->ivac/dot_general | solution.py:52
  90.2 12.6 %reshape.66 = bf16[128,2,16384]{2,1,0:T(2,128)(2,1)} reshape(bf16[128,2,128,128]{3,2,1,0:T(8,128)(2,1)} %fusion.11) | data formatting | bytes 16777216 | tf_op jit(solution)/shard_map/reshape | solution.py:55
  102.7 106.9 %all-gather.5.cloned.1.call-done = bf16[32,2,5,16384]{3,1,2,0:T(2,128)(2,1)} async-done(((bf16[4,2,5,16384]{3,1,2,0:T(2,128)(2,1)}), bf16[32,2,5,16384]{3,1,2,0:T(2,128)(2,1)}) %all-gather.5.cloned.1.call-update) | async-done | bytes 10485776 | tf_op jit(solution)/shard_map/all_gather | solution.py:68
  209.6 16.4 %fusion.28 = f32[128,32,2,5]{0,1,3,2:T(8,128)S(1)} fusion(bf16[128,2,16384,1]{2,1,0,3:T(2,128)(2,1)} %bitcast.36, bf16[32,2,5,16384]{3,1,2,0:T(2,128)(2,1)} %all-gather.5.cloned.1.call-done), kind=kOutput, calls=%fused_computation.20 | convolution fusion | flops 1342177280 | bytes 19038208 | tf_op jit(solution)/shard_map/ivx,svqx->isvq/dot_general | solution.py:65
  226.0 0.1 copy.52
  226.1 0.7 reshape.67
  226.8 3.3 %all-to-all-start = ((f32[128,4,80]{0,2,1:T(8,128)}), f32[128,4,80]{0,2,1:T(8,128)S(1)}, u32[]{:S(2)}, u32[]{:S(2)}) async-start(f32[128,4,80]{0,2,1:T(8,128)} %reshape.67), calls=%async_computation | async-start | bytes 327680 | tf_op jit(solution)/shard_map/all_to_all | solution.py:73
  230.2 4.9 %all-to-all-done = f32[128,4,80]{0,2,1:T(8,128)S(1)} async-done(((f32[128,4,80]{0,2,1:T(8,128)}), f32[128,4,80]{0,2,1:T(8,128)S(1)}, u32[]{:S(2)}, u32[]{:S(2)}) %all-to-all-start) | async-done | bytes 163872 | tf_op jit(solution)/shard_map/all_to_all | solution.py:73
  235.0 0.7 gather_fusion.2
  235.8 0.1 select_bitcast_fusion
  235.9 0.8 copy.53
  (8 shorter events, 0.1 us)
Async XLA Ops:
  6.5 52.4 %copy-start = (bf16[1024,1024]{1,0:T(8,128)(2,1)S(1)}, bf16[1024,1024]{1,0:T(8,128)(2,1)}, u32[]{:S(2)}) copy-start(bf16[1024,1024]{1,0:T(8,128)(2,1)} %param.6) | copy-start | bytes 6291460
  6.5 39.6 %all-gather.3.cloned.1.call-start = ((), (), s32[]{:S(2)}) async-start(), calls=%async_computation.1 | async-start | bytes 5242880 | tf_op jit(solution)/shard_map/all_gather | solution.py:39
  7.3 202.3 %all-gather.5.cloned.1.call-start = ((), (), s32[]{:S(2)}) async-start(), calls=%async_computation.2 | async-start | bytes 11796480 | tf_op jit(solution)/shard_map/all_gather | solution.py:68
  53.4 7.1 %copy-start.1 = (s32[1024,1]{0,1:T(1,128)S(1)}, s32[1024,1]{0,1:T(1,128)}, u32[]{:S(2)}) copy-start(s32[1024,1]{0,1:T(1,128)} %param.5) | copy-start | bytes 12292
  226.8 8.3 %all-to-all-start = ((f32[128,4,80]{0,2,1:T(8,128)}), f32[128,4,80]{0,2,1:T(8,128)S(1)}, u32[]{:S(2)}, u32[]{:S(2)}) async-start(f32[128,4,80]{0,2,1:T(8,128)} %reshape.67), calls=%async_computation | async-start | bytes 327680 | tf_op jit(solution)/shard_map/all_to_all | solution.py:73
Sparse Core Ops, SparseCore 0:
  8.9 37.1 all-gather.2
  59.0 150.4 all-gather.4
where the time goes:
time: 244 us; the launch traced here: 243 us
  waiting for transfers between devices  150 us (61%)
  local copies, waits for them, and re-layouts  40.9 us (17%)
  matrix products  34.2 us (14%)
  between operations  13.5 us (6%)
  starting transfers between devices  3.39 us (1%)
    all_gather x1, waiting for transfers between devices, shards(): lax.all_gather(routed, 'row', axis=0, tiled=True)  107 us
    all_gather x1, waiting for transfers between devices, shards(): row_coeffs = lax.all_gather(coeffs, 'col', axis=0, tiled=True)  37.6 us
    dot_general x1, matrix products, shards(): jnp.einsum('ivx,svqx->isvq', reduced, lax.all_gather(routed, 'row', axis=...  16.4 us
    dot_general x1, matrix products, shards(): jnp.einsum('ivba,vcib->ivac', product_tile, dual_pick, preferred_element_...  15 us
    reshape x1, local copies, waits for them, and re-layouts, shards(): reduced = reduced.reshape(row_count, per_col, tile_area)  12.6 us
    reshape x1, local copies, waits for them, and re-layouts, shards(): row_coeffs.reshape(col_size, own_count, tile_area)  7.31 us
    gather x1, local copies, waits for them, and re-layouts, shards(): primal_pick = jnp.take(primal_strip, row_tiles, axis=0)  6.69 us
    gather x1, local copies, waits for them, and re-layouts, shards(): dual_pick = jnp.take(dual_strip, row_tiles, axis=2)  6.68 us
  transfers between devices with their start and end apart: 3, of which 3 were waited for; matrix products, arithmetic and copies ran while one was open for 18% of the time, Pallas kernels for 0%

commit v1 on v0

--- a/solution.py
+++ b/solution.py
@@ -4,6 +4,19 @@
 from jax.sharding import PartitionSpec as P
 
 MOST = 5
+
+
+def collect(array, axis, dim):
+    ways = lax.axis_size(axis)
+    up = [(d, (d + 1) % ways) for d in range(ways)]
+    down = [(d, (d - 1) % ways) for d in range(ways)]
+    earlier, later = ([array], [array])
+    for _ in range(ways // 2):
+        earlier.append(lax.ppermute(earlier[-1], axis, up))
+    for _ in range((ways - 1) // 2):
+        later.append(lax.ppermute(later[-1], axis, down))
+    line = jnp.concatenate([*earlier[::-1], *later[1:]], axis=dim)
+    return jnp.roll(line, (lax.axis_index(axis) - ways // 2) * array.shape[dim], axis=dim)
 
 
 def slot_ranks(tile_group, first_tile, tile_width):
@@ -63,10 +76,7 @@
         preferred_element_type=jnp.float32,
     ).astype(jnp.bfloat16)
     values = jnp.einsum(
-        "ivx,svqx->isvq",
-        reduced,
-        lax.all_gather(routed, "row", axis=0, tiled=True),
-        preferred_element_type=jnp.float32,
+        "ivx,svqx->isvq", reduced, collect(routed, "row", 0), preferred_element_type=jnp.float32
     )
     home_span = row_size * per_col * slot_depth
     values = values.reshape(row_count, col_size, home_span)

time: 244 us -> 332 us (1.36)
  local copies, waits for them, and re-layouts: 40.9 us -> 74.8 us
  starting transfers between devices: 3.39 us -> 29 us
  waiting for transfers between devices: 150 us -> 169 us
  matrix products: 34.2 us -> 42.7 us
    ppermute x0 -> x7, waiting for transfers between devices: none -> 126 us  [the longest x4 110 us: collect(): earlier.append(lax.ppermute(earlier[-1], axis, up))]
    all_gather x1 -> x0, waiting for transfers between devices: 107 us -> none  [shards(): lax.all_gather(routed, 'row', axis=0, tiled=True)]
    ppermute x0 -> x7, starting transfers between devices: none -> 25.6 us  [the longest x3 19.1 us: collect(): later.append(lax.ppermute(later[-1], axis, down))]
    unnamed x6 -> x31, local copies, waits for them, and re-layouts: 1.18 us -> 25.8 us
    dot_general x1, matrix products: 16.4 us -> 24.9 us  [shards(): jnp.einsum('ivx,svqx->isvq', reduced, collect(routed, 'row', 0), preferre...]
    dynamic_slice x0 -> x1, local copies, waits for them, and re-layouts: none -> 7.41 us  [collect(): jnp.roll(line, (lax.axis_index(axis) - ways // 2) * array.shape[dim], axi...]
  transfers between devices with their start and end apart: 3 -> 9, of which waited for: 3 -> 6; matrix products, arithmetic and copies ran while one was open for 18% -> 17% of each run, Pallas kernels for 0% -> 0%
where the time goes in v1:
time: 332 us; the launch traced here: 331 us
  waiting for transfers between devices  169 us (51%)
  local copies, waits for them, and re-layouts  74.8 us (23%)
  matrix products  42.7 us (13%)
  starting transfers between devices  29 us (9%)
  between operations  13.6 us (4%)
    ppermute x4, waiting for transfers between devices, collect(): earlier.append(lax.ppermute(earlier[-1], axis, up))  110 us
    all_gather x1, waiting for transfers between devices, shards(): row_coeffs = lax.all_gather(coeffs, 'col', axis=0, tiled=True)  37.6 us
    unnamed x31, local copies, waits for them, and re-layouts  25.8 us
    dot_general x1, matrix products, shards(): jnp.einsum('ivx,svqx->isvq', reduced, collect(routed, 'row', 0), preferre...  24.9 us
    ppermute x3, starting transfers between devices, collect(): later.append(lax.ppermute(later[-1], axis, down))  19.1 us
    ppermute x3, waiting for transfers between devices, collect(): later.append(lax.ppermute(later[-1], axis, down))  16.4 us
    dot_general x1, matrix products, shards(): jnp.einsum('ivba,vcib->ivac', product_tile, dual_pick, preferred_element_...  14.9 us
    reshape x1, local copies, waits for them, and re-layouts, shards(): reduced = reduced.reshape(row_count, per_col, tile_area)  12.5 us
  transfers between devices with their start and end apart: 9, of which 6 were waited for; matrix products, arithmetic and copies ran while one was open for 17% of the time, Pallas kernels for 0%

profile of v1, /device:TPU:0, one launch (start us, length us, event | category | flops | bytes accessed | tf_op | source)
XLA Modules:
  0.0 330.8 jit_solution(8297377580957259672)
XLA Ops:
  6.5 0.7 all-gather.2.cloned.1.call-update
  7.3 0.7 fusion.41
  8.2 0.2 fusion.35
  8.5 37.6 %all-gather.2.cloned.1.call-done = bf16[128,128,128]{2,1,0:T(8,128)(2,1)} async-done(((bf16[32,128,128]{2,1,0:T(8,128)(2,1)}), bf16[128,128,128]{2,1,0:T(8,128)(2,1)}) %all-gather.2.cloned.1.call-update) | async-done | bytes 4194320 | tf_op jit(solution)/shard_map/all_gather | solution.py:52
  46.1 7.3 %reshape.93 = bf16[4,32,16384,1]{2,1,0,3:T(8,128)(2,1)} reshape(bf16[128,128,128]{2,1,0:T(8,128)(2,1)} %all-gather.2.cloned.1.call-done) | data formatting | bytes 8388608 | tf_op jit(solution)/shard_map/reshape | solution.py:75
  53.4 2.9 convolution_convert_fusion
  56.3 1.3 copy-done.2
  57.6 2.2 copy.62
  59.8 1.5 collective-permute-start
  61.3 32.4 %collective-permute-done = bf16[4,2,5,16384]{3,0,2,1:T(4,128)(2,1)S(1)} collective-permute-done((bf16[4,2,5,16384]{3,0,2,1:T(4,128)(2,1)}, bf16[4,2,5,16384]{3,0,2,1:T(4,128)(2,1)S(1)}, u32[]{:S(2)}, u32[]{:S(2)}) %collective-permute-start) | collective-permute-done | bytes 1310752 | tf_op jit(solution)/shard_map/ppermute | solution.py:15
  93.7 4.7 %collective-permute-start.4 = (bf16[4,2,5,16384]{3,0,2,1:T(4,128)(2,1)}, bf16[4,2,5,16384]{3,0,2,1:T(4,128)(2,1)}, u32[]{:S(2)}, u32[]{:S(2)}) collective-permute-start(bf16[4,2,5,16384]{3,0,2,1:T(4,128)(2,1)} %copy.62), channel_id=1, source_target_pairs={{0,28},{4,0},{8,4},{12,8},{16,12},{20,16},{24,20},{28,24},{1,29},{... | collective-permute-start | bytes 3932168 | tf_op jit(solution)/shard_map/ppermute | solution.py:17
  98.4 51.2 %collective-permute-done.1 = bf16[4,2,5,16384]{3,0,2,1:T(4,128)(2,1)} collective-permute-done((bf16[4,2,5,16384]{3,0,2,1:T(4,128)(2,1)S(1)}, bf16[4,2,5,16384]{3,0,2,1:T(4,128)(2,1)}, u32[]{:S(2)}, u32[]{:S(2)}) %collective-permute-start.1) | collective-permute-done | bytes 1310752 | tf_op jit(solution)/shard_map/ppermute | solution.py:15
  149.6 2.6 collective-permute-start.2
  152.2 0.9 constant_dynamic-slice_fusion
  153.1 1.2 reshape.97
  154.3 1.1 dynamic-slice_bitcast_fusion
  155.7 6.6 %gather_fusion = bf16[128,128,2,128]{3,1,2,0:T(8,128)(2,1)} fusion(bf16[8,128,2,128]{3,1,2,0:T(8,128)(2,1)S(1)} %copy.79, s32[1024]{0:T(1024)S(1)} %pad_clamp_fusion.1), kind=kCustom, calls=%fused_computation | custom fusion | bytes 16777728 | tf_op jit(solution)/shard_map/jit(_take)/gather | solution.py:56
  162.3 6.6 %gather_fusion.1 = bf16[128,2,128,128]{3,2,1,0:T(8,128)(2,1)} fusion(bf16[2,128,8,128]{3,1,2,0:T(8,128)(2,1)S(1)} %copy.81, s32[1024]{0:T(1024)S(1)} %pad_clamp_fusion.1), kind=kCustom, calls=%fused_computation.1 | custom fusion | bytes 16777728 | tf_op jit(solution)/shard_map/jit(_take)/gather | solution.py:64
  169.0 0.7 fusion.44
  170.1 11.4 %collective-permute-start.5 = (bf16[4,2,5,16384]{3,0,2,1:T(4,128)(2,1)}, bf16[4,2,5,16384]{3,0,2,1:T(4,128)(2,1)}, u32[]{:S(2)}, u32[]{:S(2)}) collective-permute-start(bf16[4,2,5,16384]{3,0,2,1:T(4,128)(2,1)} %collective-permute-done.4), channel_id=1, source_target_pairs={{0,28},{4,0},{8,4},{12,8},{16,12},{20,16},{24,20},{28,24},{1,29},{... | collective-permute-start | bytes 3932168 | tf_op jit(solution)/shard_map/ppermute | solution.py:17
  181.5 26.2 %collective-permute-done.2 = bf16[4,2,5,16384]{3,0,2,1:T(4,128)(2,1)} collective-permute-done((bf16[4,2,5,16384]{3,0,2,1:T(4,128)(2,1)}, bf16[4,2,5,16384]{3,0,2,1:T(4,128)(2,1)}, u32[]{:S(2)}, u32[]{:S(2)}) %collective-permute-start.2) | collective-permute-done | bytes 1310752 | tf_op jit(solution)/shard_map/ppermute | solution.py:15
  207.6 2.5 collective-permute-start.3
  210.1 14.9 %fusion.11 = bf16[128,2,128,128]{3,2,1,0:T(8,128)(2,1)} fusion(bf16[128,2,128,128]{3,2,1,0:T(8,128)(2,1)} %gather_fusion.1, pred[128]{0:T(512)(128)(4,1)S(1)} %get-tuple-element.7, bf16[128,128,2,128]{3,1,2,0:T(8,128)(2,1)} %gather_fusion, bf16[128,128,128]{2,1,0:T(8,128)(2,1)} %all-gather.2.cloned.1.call-done), kind=kOutput, calls=%fused_computation.15 | convolution fusion | flops 2164260864 | bytes 29360256 | tf_op jit(solution)/shard_map/ivba,vcib->ivac/dot_general | solution.py:65
  225.0 12.5 %reshape.66 = bf16[128,2,16384]{2,1,0:T(2,128)(2,1)} reshape(bf16[128,2,128,128]{3,2,1,0:T(8,128)(2,1)} %fusion.11) | data formatting | bytes 16777216 | tf_op jit(solution)/shard_map/reshape | solution.py:68
  237.5 3.0 collective-permute-start.6
  240.5 2.1 copy_dynamic-update-slice_fusion.12
  242.6 2.1 copy_dynamic-update-slice_fusion.10
  244.7 2.1 copy_dynamic-update-slice_fusion.8
  246.7 0.7 copy_dynamic-update-slice_fusion.6
  247.7 2.1 copy_dynamic-update-slice_fusion.4
  249.7 2.1 copy_dynamic-update-slice_fusion.2
  251.8 16.4 %collective-permute-done.6 = bf16[4,2,5,16384]{3,0,2,1:T(4,128)(2,1)S(1)} collective-permute-done((bf16[4,2,5,16384]{3,0,2,1:T(4,128)(2,1)}, bf16[4,2,5,16384]{3,0,2,1:T(4,128)(2,1)S(1)}, u32[]{:S(2)}, u32[]{:S(2)}) %collective-permute-start.6) | collective-permute-done | bytes 1310752 | tf_op jit(solution)/shard_map/ppermute | solution.py:17
  268.2 0.7 copy_dynamic-update-slice_fusion
  269.0 2.1 copy_dynamic-update-slice_fusion.13
  271.0 2.1 copy_dynamic-update-slice_fusion.11
  273.1 2.1 copy_dynamic-update-slice_fusion.9
  275.2 0.7 copy_dynamic-update-slice_fusion.7
  275.9 0.1 constant_dynamic-update-slice_fusion
  276.1 2.1 copy_dynamic-update-slice_fusion.5
  278.2 2.1 copy_dynamic-update-slice_fusion.3
  280.2 0.7 copy_dynamic-update-slice_fusion.1
  281.0 7.4 %constant_dynamic-slice_fusion.1 = bf16[32,2,5,16384]{3,2,1,0:T(8,128)(2,1)} fusion(bf16[64,2,5,16384]{3,2,1,0:T(8,128)(2,1)S(1)} %copy_dynamic-update-slice_fusion.1, s32[]{:T(128)S(6)} %select_n.62), kind=kLoop, calls=%fused_computation.64 | loop fusion | bytes 20971524 | tf_op jit(solution)/shard_map/jit(_roll_dynamic)/dynamic_slice | solution.py:19
  288.4 24.9 %fusion.28 = f32[128,32,2,5]{0,1,3,2:T(8,128)S(1)} fusion(bf16[128,2,16384,1]{2,1,0,3:T(2,128)(2,1)S(1)} %bitcast.38, bf16[32,2,5,16384]{3,2,1,0:T(8,128)(2,1)} %constant_dynamic-slice_fusion.1), kind=kOutput, calls=%fused_computation.34 | convolution fusion | flops 1342177280 | bytes 19038208 | tf_op jit(solution)/shard_map/ivx,svqx->isvq/dot_general | solution.py:78
  313.4 0.7 reshape.67
  314.1 3.3 %all-to-all-start = ((f32[128,4,80]{0,2,1:T(8,128)}), f32[128,4,80]{0,2,1:T(8,128)S(1)}, u32[]{:S(2)}, u32[]{:S(2)}) async-start(f32[128,4,80]{0,2,1:T(8,128)} %reshape.67), calls=%async_computation | async-start | bytes 327680 | tf_op jit(solution)/shard_map/all_to_all | solution.py:83
  317.5 4.9 %all-to-all-done = f32[128,4,80]{0,2,1:T(8,128)S(1)} async-done(((f32[128,4,80]{0,2,1:T(8,128)}), f32[128,4,80]{0,2,1:T(8,128)S(1)}, u32[]{:S(2)}, u32[]{:S(2)}) %all-to-all-start) | async-done | bytes 163872 | tf_op jit(solution)/shard_map/all_to_all | solution.py:83
  322.4 0.7 gather_fusion.2
  323.2 0.8 copy.85
  (43 shorter events, 1.6 us)
Async XLA Ops:
  6.5 145.7 %copy-start = (bf16[1024,1024]{1,0:T(8,128)(2,1)S(1)}, bf16[1024,1024]{1,0:T(8,128)(2,1)}, u32[]{:S(2)}) copy-start(bf16[1024,1024]{1,0:T(8,128)(2,1)} %param.6) | copy-start | bytes 6291460
  6.5 39.6 %all-gather.2.cloned.1.call-start = ((), (), s32[]{:S(2)}) async-start(), calls=%async_computation.1 | async-start | bytes 5242880 | tf_op jit(solution)/shard_map/all_gather | solution.py:52
  53.4 102.2 %copy-start.4 = (s32[1024,1]{0,1:T(1,128)S(1)}, s32[1024,1]{0,1:T(1,128)}, u32[]{:S(2)}) copy-start(s32[1024,1]{0,1:T(1,128)} %param.5) | copy-start | bytes 12292
  56.3 1.3 copy-start.2
  59.8 33.8 %collective-permute-start = (bf16[4,2,5,16384]{3,0,2,1:T(4,128)(2,1)}, bf16[4,2,5,16384]{3,0,2,1:T(4,128)(2,1)S(1)}, u32[]{:S(2)}, u32[]{:S(2)}) collective-permute-start(bf16[4,2,5,16384]{3,0,2,1:T(4,128)(2,1)} %copy.62), channel_id=1, source_target_pairs={{0,4},{4,8},{8,12},{12,16},{16,20},{20,24},{24,28},{28,0},{1,5},{5... | collective-permute-start | bytes 3932168 | tf_op jit(solution)/shard_map/ppermute | solution.py:15
  93.7 56.0 %collective-permute-start.1 = (bf16[4,2,5,16384]{3,0,2,1:T(4,128)(2,1)S(1)}, bf16[4,2,5,16384]{3,0,2,1:T(4,128)(2,1)}, u32[]{:S(2)}, u32[]{:S(2)}) collective-permute-start(bf16[4,2,5,16384]{3,0,2,1:T(4,128)(2,1)S(1)} %collective-permute-done), channel_id=1, source_target_pairs={{0,4},{4,8},{8,12},{12,16},{16,20},{20,24},{24,28},{28,0},{1,5},{5... | collective-permute-start | bytes 3932168 | tf_op jit(solution)/shard_map/ppermute | solution.py:15
  93.7 76.4 %collective-permute-start.4 = (bf16[4,2,5,16384]{3,0,2,1:T(4,128)(2,1)}, bf16[4,2,5,16384]{3,0,2,1:T(4,128)(2,1)}, u32[]{:S(2)}, u32[]{:S(2)}) collective-permute-start(bf16[4,2,5,16384]{3,0,2,1:T(4,128)(2,1)} %copy.62), channel_id=1, source_target_pairs={{0,28},{4,0},{8,4},{12,8},{16,12},{20,16},{24,20},{28,24},{1,29},{... | collective-permute-start | bytes 3932168 | tf_op jit(solution)/shard_map/ppermute | solution.py:17
  149.6 58.0 %collective-permute-start.2 = (bf16[4,2,5,16384]{3,0,2,1:T(4,128)(2,1)}, bf16[4,2,5,16384]{3,0,2,1:T(4,128)(2,1)}, u32[]{:S(2)}, u32[]{:S(2)}) collective-permute-start(bf16[4,2,5,16384]{3,0,2,1:T(4,128)(2,1)} %collective-permute-done.1), channel_id=1, source_target_pairs={{0,4},{4,8},{8,12},{12,16},{16,20},{20,24},{24,28},{28,0},{1,5},{5... | collective-permute-start | bytes 3932168 | tf_op jit(solution)/shard_map/ppermute | solution.py:15
  170.1 67.4 %collective-permute-start.5 = (bf16[4,2,5,16384]{3,0,2,1:T(4,128)(2,1)}, bf16[4,2,5,16384]{3,0,2,1:T(4,128)(2,1)}, u32[]{:S(2)}, u32[]{:S(2)}) collective-permute-start(bf16[4,2,5,16384]{3,0,2,1:T(4,128)(2,1)} %collective-permute-done.4), channel_id=1, source_target_pairs={{0,28},{4,0},{8,4},{12,8},{16,12},{20,16},{24,20},{28,24},{1,29},{... | collective-permute-start | bytes 3932168 | tf_op jit(solution)/shard_map/ppermute | solution.py:17
  207.6 32.9 %collective-permute-start.3 = (bf16[4,2,5,16384]{3,0,2,1:T(4,128)(2,1)}, bf16[4,2,5,16384]{3,0,2,1:T(4,128)(2,1)}, u32[]{:S(2)}, u32[]{:S(2)}) collective-permute-start(bf16[4,2,5,16384]{3,0,2,1:T(4,128)(2,1)} %collective-permute-done.2), channel_id=1, source_target_pairs={{0,4},{4,8},{8,12},{12,16},{16,20},{20,24},{24,28},{28,0},{1,5},{5... | collective-permute-start | bytes 3932168 | tf_op jit(solution)/shard_map/ppermute | solution.py:15
  237.5 10.0 %copy-start.3 = (bf16[4,2,5,16384]{3,2,1,0:T(8,128)(2,1)S(1)}, bf16[4,2,5,16384]{3,2,1,0:T(8,128)(2,1)}, u32[]{:S(2)}) copy-start(bf16[4,2,5,16384]{3,2,1,0:T(8,128)(2,1)} %copy-done.2) | copy-start | bytes 3932164
  237.5 30.7 %collective-permute-start.6 = (bf16[4,2,5,16384]{3,0,2,1:T(4,128)(2,1)}, bf16[4,2,5,16384]{3,0,2,1:T(4,128)(2,1)S(1)}, u32[]{:S(2)}, u32[]{:S(2)}) collective-permute-start(bf16[4,2,5,16384]{3,0,2,1:T(4,128)(2,1)} %collective-permute-done.5), channel_id=1, source_target_pairs={{0,28},{4,0},{8,4},{12,8},{16,12},{20,16},{24,20},{28,24},{1,29},{... | collective-permute-start | bytes 3932168 | tf_op jit(solution)/shard_map/ppermute | solution.py:17
  280.2 8.2 %slice-start = ((s8[8388608]{0:T(1024)(128)(4,1)}), s8[4194304]{0:T(1024)(128)(4,1)S(1)}, s32[]{:S(2)}) async-start(s8[8388608]{0:T(1024)(128)(4,1)} %bitcast.36), calls=%async_computation.2 | async-start | bytes 8388608
  281.0 7.4 %slice-start.1 = ((s8[8388608]{0:T(1024)(128)(4,1)}), s8[4194304]{0:T(1024)(128)(4,1)S(1)}, s32[]{:S(2)}) async-start(s8[8388608]{0:T(1024)(128)(4,1)} %bitcast.36), calls=%async_computation.3 | async-start | bytes 8388608
  288.4 35.6 %copy-start.1 = (bf16[1024,1024]{1,0:T(8,128)(2,1)S(1)}, bf16[1024,1024]{1,0:T(8,128)(2,1)}, u32[]{:S(2)}) copy-start(bf16[1024,1024]{1,0:T(8,128)(2,1)} %param.6) | copy-start | bytes 6291460
  314.1 8.3 %all-to-all-start = ((f32[128,4,80]{0,2,1:T(8,128)}), f32[128,4,80]{0,2,1:T(8,128)S(1)}, u32[]{:S(2)}, u32[]{:S(2)}) async-start(f32[128,4,80]{0,2,1:T(8,128)} %reshape.67), calls=%async_computation | async-start | bytes 327680 | tf_op jit(solution)/shard_map/all_to_all | solution.py:83
Sparse Core Ops, SparseCore 0:
  8.9 37.1 all-gather.1
